TPU v7x, 32 devices: a whole 2x2x4 slice. The times are simulated.
32 devices in a mesh: row: 8 (over z, x), col: 4 (over y, core).
Axes of the slice: x: 2, y: 2, z: 4, core: 2. Of those that a mesh axis runs over, the one named last changes fastest.
Arguments:
- lower: bfloat16 [8, 3, 512, 2, 512], P('row', None, None, None, 'col'), as said below
- rhs: bfloat16 [8, 3, 512, 8192], P('row', None, None, 'col'), may hold values from -6 to 6
- tile_map: int32 [16], replicated, may hold values from 0 to 15, each once
Outputs:
- overwritten: bfloat16 [8, 3, 512, 8192], P('row', None, None, 'col')
Inputs may be any that keep to these rules, and one draw needn't show every extreme that they name: tile_map is a permutation of 0 to 15. lower[0, 0, :, 0, :] and lower[1, 0, :, 1, :] are lower triangular with diagonal entries between 2 and 3; lower[0, 0, :, 1, :] is zero.
All inputs are finite; a program needn't handle non-finite values.
Results may differ from a plain program's by a relative error of at most 0.0032.
Values may be sent and summed in bfloat16 or wider, within the bound.
A program may use at most 128 MiB of HBM per device.

v0:
```python
import jax
import jax.numpy as jnp
from jax import lax
from jax.sharding import PartitionSpec as P


def from_root(value, axis, source):
    kept = jnp.where(lax.axis_index(axis) == source, value, 0).astype(value.dtype)
    return lax.psum(kept, axis)


def reorder(block, tile_map, tile):
    shape = block.shape
    tiles = block.reshape(shape[:-1] + (shape[-1] // tile, tile))
    return jnp.take(tiles, tile_map, axis=3).reshape(shape)


def body(lower, rhs, tile_map):
    tile = lower.shape[2]
    here = lax.axis_index("row")
    whole = lax.all_gather(lower, "col", axis=4, tiled=True)
    panels = whole[0]
    rows = panels.shape[0] * tile
    rhs = lax.all_to_all(
        reorder(
            lax.all_to_all(rhs, "col", split_axis=2, concat_axis=3, tiled=True), tile_map, tile
        ),
        "col",
        split_axis=3,
        concat_axis=2,
        tiled=True,
    )
    work = rhs[0].astype(jnp.float32)
    identity = jnp.eye(tile, dtype=jnp.float32)
    solved_rows = []
    for panel in range(2):
        mine = jnp.where(
            here == panel, jnp.tril(panels[0, :, panel, :].astype(jnp.float32)), identity
        )
        local = jax.scipy.linalg.solve_triangular(mine, work[0], lower=True).astype(jnp.bfloat16)
        solved = from_root(local, "row", panel)
        flat = panels[:, :, panel, :].reshape(rows, tile)
        work = work - jnp.dot(flat, solved, preferred_element_type=jnp.float32).reshape(work.shape)
        solved_rows.append(solved)
    first, second = (solved_rows[0], solved_rows[1])
    result = work.astype(jnp.bfloat16)
    leading = jnp.where(here == 0, first, jnp.where(here == 1, second, result[0]))
    result = result.at[0].set(leading)[None]
    return result


def solution(mesh):
    placed = (P("row", None, None, None, "col"), P("row", None, None, "col"), P())
    return jax.shard_map(
        body, mesh=mesh, in_specs=placed, out_specs=P("row", None, None, "col"), check_vma=False
    )
```

profile of v0, /device:TPU:25, one launch (start us, length us, event | category | flops | bytes accessed | tf_op | source)
XLA Modules:
  0.0 614.1 jit_solution(11113632346526701513)
XLA Ops:
  6.5 11.4 %copy.15 = bf16[1,3,512,2048]{3,1,0,2:T(4,128)(2,1)} copy(bf16[1,3,512,2048]{3,2,1,0:T(8,128)(2,1)} %param.8) | data formatting | bytes 12582912 | tf_op args[1]
  17.9 6.4 %all-to-all-start = ((bf16[1,3,512,2048]{3,1,0,2:T(4,128)(2,1)}), bf16[1,3,512,2048]{3,1,0,2:T(4,128)(2,1)}, u32[]{:S(2)}, u32[]{:S(2)}) async-start(bf16[1,3,512,2048]{3,1,0,2:T(4,128)(2,1)} %copy.15), calls=%async_computation | async-start | bytes 16777216 | tf_op jit(solution)/shard_map/all_to_all | solution.py:26
  26.0 107.4 %all-to-all-done = bf16[1,3,512,2048]{3,1,0,2:T(4,128)(2,1)} async-done(((bf16[1,3,512,2048]{3,1,0,2:T(4,128)(2,1)}), bf16[1,3,512,2048]{3,1,0,2:T(4,128)(2,1)}, u32[]{:S(2)}, u32[]{:S(2)}) %all-to-all-start) | async-done | bytes 6291488 | tf_op jit(solution)/shard_map/all_to_all | solution.py:26
  133.4 10.6 %copy.16 = bf16[1,3,512,2048]{3,2,1,0:T(8,128)(2,1)} copy(bf16[1,3,512,2048]{3,1,0,2:T(4,128)(2,1)} %all-to-all-done) | data formatting | bytes 12582912 | tf_op jit(solution)/shard_map/all_to_all | solution.py:26
  144.0 8.7 %copy.17 = bf16[1,3,128,4,2048]{2,4,3,1,0:T(8,128)(2,1)} copy(bf16[1,3,128,4,2048]{4,2,3,1,0:T(8,128)(2,1)} %bitcast.121) | data formatting | bytes 12582912 | tf_op jit(solution)/shard_map/all_to_all | solution.py:26
  152.7 8.6 %copy.18 = bf16[3,128,16,512]{3,1,2,0:T(8,128)(2,1)} copy(bf16[3,128,16,512]{1,3,2,0:T(8,128)(2,1)} %bitcast.122) | data formatting | bytes 12582912 | tf_op jit(solution)/shard_map/reshape | solution.py:14
  161.3 6.4 %gather_fusion = bf16[16,3,128,512]{3,2,1,0:T(8,128)(2,1)} fusion(bf16[3,128,16,512]{3,1,2,0:T(8,128)(2,1)} %copy.18, s32[1024]{0:T(1024)S(1)} %pad_clamp_fusion), kind=kCustom, calls=%fused_computation | custom fusion | bytes 12582976 | tf_op jit(solution)/shard_map/jit(_take)/gather | solution.py:15
  167.7 8.6 %copy.19 = bf16[3,128,16,512]{1,3,2,0:T(8,128)(2,1)} copy(bf16[3,128,16,512]{3,1,0,2:T(8,128)(2,1)} %bitcast.120) | data formatting | bytes 12582912 | tf_op jit(solution)/shard_map/jit(_take)/gather | solution.py:15
  176.3 4.1 bitcast_select_fusion
  180.4 39.9 %copy.20 = bf16[1,3,128,8192]{2,1,0,3:T(4,128)(2,1)} copy(bf16[1,3,128,8192]{2,3,1,0:T(8,128)(2,1)S(1)} %bitcast_select_fusion) | data formatting | bytes 12582912 | tf_op jit(solution)/shard_map/jit(_take)/select_n | solution.py:15
  220.3 6.6 %all-to-all-start.1 = ((bf16[1,3,128,8192]{2,1,0,3:T(4,128)(2,1)}), bf16[1,3,128,8192]{2,1,0,3:T(4,128)(2,1)}, u32[]{:S(2)}, u32[]{:S(2)}) async-start(bf16[1,3,128,8192]{2,1,0,3:T(4,128)(2,1)} %copy.20), calls=%async_computation.1 | async-start | bytes 16777216 | tf_op jit(solution)/shard_map/all_to_all | solution.py:24
  227.2 2.5 fusion.35
  229.7 8.1 %while.5 = (s32[]{:T(128)}, f32[512,512]{1,0:T(8,128)S(1)}, s32[4,2]{0,1:T(2,128)S(1)}, f32[4,128,128]{2,1,0:T(8,128)S(1)}, s32[]{:T(128)}) while((s32[]{:T(128)}, f32[512,512]{1,0:T(8,128)S(1)}, s32[4,2]{0,1:T(2,128)S(1)}, f32[4,128,128]{2,1,0:T(8,128)S(1)}, s32[]{:T(128)}) %tuple.41), condition=%wide.while_cond.1, body=%wide.while_body.1.sunk | while | flops 2 | bytes 131189 | solution.py:40
  237.8 39.3 %custom-call.4 = f32[4,128,128]{1,2,0:T(8,128)S(1)} custom-call(f32[4,128,128]{2,1,0:T(8,128)S(1)} %get-tuple-element.32), custom_call_target="InvertDiagBlocksLowerTriangular" | custom-call | tf_op jit(solution)/shard_map/jit(_solve_triangular)/triangular_solve | solution.py:40
  277.1 42.0 %all-to-all-done.1 = bf16[1,3,128,8192]{2,1,0,3:T(4,128)(2,1)} async-done(((bf16[1,3,128,8192]{2,1,0,3:T(4,128)(2,1)}), bf16[1,3,128,8192]{2,1,0,3:T(4,128)(2,1)}, u32[]{:S(2)}, u32[]{:S(2)}) %all-to-all-start.1) | async-done | bytes 6291488 | tf_op jit(solution)/shard_map/all_to_all | solution.py:24
  319.2 4.3 copy.21
  324.6 4.6 copy-done.1
  331.4 5.4 copy.24
  336.9 2.4 fusion.38
  345.9 3.0 fusion.18
  351.8 11.6 %while.6 = (s32[]{:T(128)}, f32[512,512]{1,0:T(8,128)}, s32[4,2]{0,1:T(2,128)S(1)}, f32[4,128,128]{2,1,0:T(8,128)S(1)}, s32[]{:T(128)}) while((s32[]{:T(128)}, f32[512,512]{1,0:T(8,128)}, s32[4,2]{0,1:T(2,128)S(1)}, f32[4,128,128]{2,1,0:T(8,128)S(1)}, s32[]{:T(128)}) %tuple.53), condition=%wide.while_cond.1.clone, body=%wide.while_body.1.clone.sunk | while | flops 2 | bytes 131189 | solution.py:40
  364.1 40.1 %custom-call.5 = f32[4,128,128]{1,2,0:T(8,128)S(1)} custom-call(f32[4,128,128]{2,1,0:T(8,128)} %copy-done.11), custom_call_target="InvertDiagBlocksLowerTriangular" | custom-call | tf_op jit(solution)/shard_map/jit(_solve_triangular)/triangular_solve | solution.py:40
  406.1 12.7 %copy.22 = f32[1,3,4,128,2048]{4,3,2,1,0:T(8,128)} copy(f32[1,3,4,128,2048]{3,4,2,1,0:T(8,128)} %copy-done.1) | data formatting | bytes 25165824 | tf_op jit(solution)/shard_map/convert_element_type | solution.py:33
  418.8 33.9 %all-reduce.3.cloned.1.call-done = bf16[512,2048]{1,0:T(8,128)(2,1)} async-done(((bf16[512,2048]{1,0:T(8,128)(2,1)}), bf16[512,2048]{1,0:T(8,128)(2,1)}) %all-reduce.3.cloned.1.call-update) | async-done | bytes 2097168 | tf_op jit(solution)/shard_map/psum | solution.py:9
  452.7 5.2 fusion.59
  458.0 6.9 %sub.25 = f32[3,512,2048]{2,1,0:T(8,128)} subtract(f32[3,512,2048]{2,1,0:T(8,128)S(1)} %bitcast.117, f32[3,512,2048]{2,1,0:T(8,128)S(1)} %bitcast.118) | non-fusion elementwise | flops 3145728 | bytes 37748736 | tf_op jit(solution)/shard_map/sub | solution.py:43
  466.2 2.5 slice_bitcast_fusion
  475.9 3.0 fusion.15
  481.7 101.7 %all-reduce.5.cloned.1.call-done = bf16[512,2048]{1,0:T(8,128)(2,1)} async-done(((bf16[512,2048]{1,0:T(8,128)(2,1)}), bf16[512,2048]{1,0:T(8,128)(2,1)}) %all-reduce.5.cloned.1.call-update) | async-done | bytes 2097168 | tf_op jit(solution)/shard_map/psum | solution.py:9
  583.4 5.1 fusion.60
  588.6 13.5 %fusion.1 = bf16[1,3,512,2048]{3,2,1,0:T(8,128)(2,1)} fusion(f32[1,3,512,2048]{3,2,1,0:T(8,128)S(1)} %bitcast.124, f32[1,3,512,2048]{3,2,1,0:T(8,128)} %bitcast.119, f32[1,3,4,128,2048]{4,3,2,1,0:T(8,128)} %copy.22), kind=kLoop, calls=%fused_computation.8 | loop fusion | flops 9437184 | bytes 44040192 | tf_op jit(solution)/shard_map/convert_element_type | solution.py:46
  602.0 5.0 fusion.27
  (82 shorter events, 48.0 us)
Async XLA Ops:
  17.9 6.9 %copy-start.10 = (bf16[1,3,512,2,128]{4,3,2,1,0:T(2,128)(2,1)S(1)}, bf16[1,3,512,2,128]{4,3,2,1,0:T(2,128)(2,1)}, u32[]{:S(2)}) copy-start(bf16[1,3,512,2,128]{4,3,2,1,0:T(2,128)(2,1)} %param.7) | copy-start | bytes 2359300
  17.9 8.0 %copy-start.12 = (s32[16]{0:T(128)S(1)}, s32[16]{0:T(128)}, u32[]{:S(2)}) copy-start(s32[16]{0:T(128)} %param.9) | copy-start | bytes 196
  17.9 115.5 %all-to-all-start = ((bf16[1,3,512,2048]{3,1,0,2:T(4,128)(2,1)}), bf16[1,3,512,2048]{3,1,0,2:T(4,128)(2,1)}, u32[]{:S(2)}, u32[]{:S(2)}) async-start(bf16[1,3,512,2048]{3,1,0,2:T(4,128)(2,1)} %copy.15), calls=%async_computation | async-start | bytes 16777216 | tf_op jit(solution)/shard_map/all_to_all | solution.py:26
  24.3 202.9 %all-gather.2.cloned.1.call-start = ((), (), s32[]{:S(2)}) async-start(), calls=%async_computation.2 | async-start | bytes 3932160 | tf_op jit(solution)/shard_map/all_gather | solution.py:21
  220.3 98.8 %all-to-all-start.1 = ((bf16[1,3,128,8192]{2,1,0,3:T(4,128)(2,1)}), bf16[1,3,128,8192]{2,1,0,3:T(4,128)(2,1)}, u32[]{:S(2)}, u32[]{:S(2)}) async-start(bf16[1,3,128,8192]{2,1,0,3:T(4,128)(2,1)} %copy.20), calls=%async_computation.1 | async-start | bytes 16777216 | tf_op jit(solution)/shard_map/all_to_all | solution.py:24
  226.9 225.8 %all-reduce.3.cloned.1.call-start = ((), (), s32[]{:S(2)}) async-start(), calls=%async_computation.3 | async-start | bytes 4194304 | tf_op jit(solution)/shard_map/psum | solution.py:9
  237.8 39.3 %copy-start.5 = (f32[512,512]{1,0:T(8,128)}, f32[512,512]{1,0:T(8,128)S(1)}, u32[]{:S(2)}) copy-start(f32[512,512]{1,0:T(8,128)S(1)} %get-tuple-element.161) | copy-start | bytes 3145732
  324.6 4.6 copy-start.1
  336.9 5.8 copy-start.3
  349.9 54.3 %copy-start.4 = (bf16[1,3,512,2,512]{4,2,3,1,0:T(8,128)(2,1)S(1)}, bf16[1,3,512,2,512]{4,2,3,1,0:T(8,128)(2,1)}, u32[]{:S(2)}) copy-start(bf16[1,3,512,2,512]{4,2,3,1,0:T(8,128)(2,1)} %all-gather.2.cloned.1.call-done) | copy-start | bytes 9437188
  351.7 231.7 %all-reduce.5.cloned.1.call-start = ((), (), s32[]{:S(2)}) async-start(), calls=%async_computation.4 | async-start | bytes 4194304 | tf_op jit(solution)/shard_map/psum | solution.py:9
  363.4 0.7 copy-start.11
  406.1 46.7 %copy-start.9 = (bf16[3,512,1,512]{3,1,2,0:T(8,128)(2,1)S(1)}, bf16[3,512,1,512]{3,1,2,0:T(8,128)(2,1)}, u32[]{:S(2)}) copy-start(bf16[3,512,1,512]{3,1,2,0:T(8,128)(2,1)} %get-tuple-element.56) | copy-start | bytes 4718596
  452.7 5.2 copy-start
  457.9 8.3 %copy-start.2 = (f32[2048,1536]{0,1:T(8,128)}, f32[2048,1536]{0,1:T(8,128)S(1)}, u32[]{:S(2)}) copy-start(f32[2048,1536]{0,1:T(8,128)S(1)} %fusion.59) | copy-start | bytes 37748740
  479.9 103.5 %copy-start.8 = (bf16[3,512,1,512]{3,1,2,0:T(8,128)(2,1)S(1)}, bf16[3,512,1,512]{3,1,2,0:T(8,128)(2,1)}, u32[]{:S(2)}) copy-start(bf16[3,512,1,512]{3,1,2,0:T(8,128)(2,1)} %get-tuple-element.57) | copy-start | bytes 4718596
  588.6 13.5 %copy-start.6 = (bf16[512,2048]{1,0:T(8,128)(2,1)S(1)}, bf16[512,2048]{1,0:T(8,128)(2,1)}, u32[]{:S(2)}) copy-start(bf16[512,2048]{1,0:T(8,128)(2,1)} %all-reduce.3.cloned.1.call-done) | copy-start | bytes 6291460
  588.6 13.5 %copy-start.7 = (bf16[512,2048]{1,0:T(8,128)(2,1)S(1)}, bf16[512,2048]{1,0:T(8,128)(2,1)}, u32[]{:S(2)}) copy-start(bf16[512,2048]{1,0:T(8,128)(2,1)} %all-reduce.5.cloned.1.call-done) | copy-start | bytes 6291460
Sparse Core Ops, SparseCore 0:
  26.7 47.0 all-gather.1
  351.8 100.8 all-reduce.2
  481.8 101.5 all-reduce.4
where the time goes:
time: 624 us; the launch traced here: 614 us
  waiting for transfers between devices  285 us (46%)
  local copies, waits for them, and re-layouts  150 us (24%)
  other arithmetic  116 us (19%)
  matrix products  34.4 us (6%)
  between operations  14 us (2%)
  starting transfers between devices  13.7 us (2%)
    psum x2, waiting for transfers between devices, from_root(): return lax.psum(kept, axis)  136 us
    all_to_all x1, waiting for transfers between devices, body(): lax.all_to_all(rhs, 'col', split_axis=2, concat_axis=3, tiled=True)  107 us
    another operation x4, other arithmetic, body(): jax.scipy.linalg.solve_triangular(mine, work[0], lower=True)  81.9 us
    all_to_all x1, waiting for transfers between devices, body(): lax.all_to_all(reorder(lax.all_to_all(rhs, 'col', split_axis=2, concat_ax...  42 us
    select_n x1, local copies, waits for them, and re-layouts, reorder(): return jnp.take(tiles, tile_map, axis=3).reshape(shape)  39.9 us
    another operation x14, matrix products, body(): jax.scipy.linalg.solve_triangular(mine, work[0], lower=True)  24.1 us
    another operation x27, local copies, waits for them, and re-layouts, body(): jax.scipy.linalg.solve_triangular(mine, work[0], lower=True)  19.4 us
    all_to_all x2, local copies, waits for them, and re-layouts, body(): lax.all_to_all(rhs, 'col', split_axis=2, concat_axis=3, tiled=True)  19.3 us
  transfers between devices with their start and end apart: 5, of which 4 were waited for; matrix products, arithmetic and copies ran while one was open for 33% of the time, Pallas kernels for 0%

commit v1 on v0

v1 whole, which is shorter than its diff:
```python
import functools

import jax
import jax.numpy as jnp
from jax import lax
from jax.experimental import pallas as pl
from jax.experimental.pallas import tpu as pltpu
from jax.sharding import PartitionSpec as P

F32 = jnp.float32
BF16 = jnp.bfloat16
ANY = pl.BlockSpec(memory_space=pl.ANY)
VMEM_LIMIT = 56 * 1024 * 1024
CHUNKS = 16
BLOCK = 128


def signal(sem, **where):
    pl.semaphore_signal(sem, inc=1, device_id=where, device_id_type=pl.DeviceIdType.MESH)


def remote(src, dst, send, recv, **where):
    return pltpu.make_async_remote_copy(
        src_ref=src,
        dst_ref=dst,
        send_sem=send,
        recv_sem=recv,
        device_id=where,
        device_id_type=pl.DeviceIdType.MESH,
    )


def spread_kernel(n, rhs, mid, bounce, send, recv, local):
    me = lax.axis_index("col")
    layers, tile, width = rhs.shape
    part = tile // n
    barrier = pltpu.get_barrier_semaphore()
    for d in range(1, n):
        signal(barrier, col=lax.rem(me + d, n))
    pl.semaphore_wait(barrier, n - 1)

    def copy(m, d):
        to = lax.rem(me + d, n)
        return remote(
            rhs.at[m, pl.ds(to * part, part)],
            mid.at[m, :, pl.ds(me * width, width)],
            send.at[m, d - 1],
            recv.at[m, d - 1],
            col=to,
        )

    for m in range(layers):
        for d in range(1, n):
            copy(m, d).start()
    first = pltpu.make_async_copy(rhs.at[:, pl.ds(me * part, part)], bounce, local.at[0])
    first.start()
    first.wait()
    second = pltpu.make_async_copy(bounce, mid.at[:, :, pl.ds(me * width, width)], local.at[1])
    second.start()
    second.wait()
    for m in range(layers):
        for d in range(1, n):
            copy(m, d).wait_recv()
    for m in range(layers):
        for d in range(1, n):
            copy(m, d).wait_send()


def spread(n, rhs):
    layers, tile, width = rhs.shape
    part = tile // n
    return pl.pallas_call(
        functools.partial(spread_kernel, n),
        out_shape=jax.ShapeDtypeStruct((layers, part, width * n), rhs.dtype),
        in_specs=[ANY],
        out_specs=ANY,
        scratch_shapes=[
            pltpu.VMEM((layers, part, width), rhs.dtype),
            pltpu.SemaphoreType.DMA((layers, n - 1)),
            pltpu.SemaphoreType.DMA((layers, n - 1)),
            pltpu.SemaphoreType.DMA((2,)),
        ],
        compiler_params=pltpu.CompilerParams(collective_id=0, has_side_effects=True),
        name="spread",
    )(rhs)


def permute_kernel(order, src, dst):
    dst[...] = src[...]


def permute(mid, tile_map, tile):
    layers, part, width = mid.shape
    return pl.pallas_call(
        permute_kernel,
        out_shape=jax.ShapeDtypeStruct(mid.shape, mid.dtype),
        grid_spec=pltpu.PrefetchScalarGridSpec(
            num_scalar_prefetch=1,
            grid=(width // tile,),
            in_specs=[pl.BlockSpec((layers, part, tile), lambda j, order: (0, 0, order[j]))],
            out_specs=pl.BlockSpec((layers, part, tile), lambda j, order: (0, 0, j)),
        ),
        name="permute",
    )(tile_map, mid)


def collect_kernel(n, n_row, nx, mid, out, cast, bounce, hold, send, recv, zsend, xsend, crecv, local):
    me = lax.axis_index("col")
    row = lax.axis_index("row")
    nz = n_row // nx
    z, x = row // nx, lax.rem(row, nx)
    layers, tile, width = out.shape
    part = tile // n
    step = tile // CHUNKS
    barrier = pltpu.get_barrier_semaphore()
    for d in range(1, n):
        signal(barrier, col=lax.rem(me + d, n))
    for d in range(1, nx):
        signal(barrier, row=z * nx + lax.rem(x + d, nx))
    for d in (1, nz - 1):
        signal(barrier, row=lax.rem(z + d, nz) * nx + x)
    pl.semaphore_wait(barrier, n + nx)

    def copy(m, d):
        to = lax.rem(me + d, n)
        return remote(
            mid.at[m, :, pl.ds(to * width, width)],
            out.at[m, pl.ds(me * part, part)],
            send.at[m, d - 1],
            recv.at[m, d - 1],
            col=to,
        )

    for m in range(layers):
        for d in range(1, n):
            copy(m, d).start()
    first = pltpu.make_async_copy(mid.at[:, :, pl.ds(me * width, width)], bounce, local.at[0])
    first.start()
    first.wait()
    second = pltpu.make_async_copy(bounce, out.at[:, pl.ds(me * part, part)], local.at[1])
    second.start()
    second.wait()
    for d in range(1, n):
        copy(0, d).wait_recv()

    @pl.when(row < 2)
    def _():
        load = pltpu.make_async_copy(out.at[0], hold, local.at[2])
        load.start()
        load.wait()
        store = pltpu.make_async_copy(hold, cast.at[row], local.at[3])
        store.start()
        store.wait()

    def down(k, c):
        piece = cast.at[k, pl.ds(c * step, step)]
        return remote(
            piece, piece, zsend.at[c], crecv.at[k, c], row=lax.rem(z + 1, nz) * nx + x
        )

    def across(k, c, d):
        piece = cast.at[k, pl.ds(c * step, step)]
        return remote(
            piece, piece, xsend.at[c, d - 1], crecv.at[k, c], row=z * nx + lax.rem(x + d, nx)
        )

    for k in range(2):

        @pl.when(x == k)
        def _(k=k):
            @pl.loop(0, CHUNKS)
            def _(c):
                @pl.when(z > 0)
                def _():
                    down(k, c).wait_recv()

                @pl.when(z < nz - 1)
                def _():
                    down(k, c).start()

                for d in range(1, nx):
                    across(k, c, d).start()

    for k in range(2):

        @pl.when(x != k)
        def _(k=k):
            @pl.loop(0, CHUNKS)
            def _(c):
                down(k, c).wait_recv()

        @pl.when(x == k)
        def _(k=k):
            @pl.loop(0, CHUNKS)
            def _(c):
                @pl.when(z < nz - 1)
                def _():
                    down(k, c).wait_send()

                for d in range(1, nx):
                    across(k, c, d).wait_send()

    for m in range(1, layers):
        for d in range(1, n):
            copy(m, d).wait_recv()
    for m in range(layers):
        for d in range(1, n):
            copy(m, d).wait_send()


def collect(n, n_row, mid, tile):
    layers, part, total = mid.shape
    width = total // n
    nx = 2
    while nx * nx * 4 <= n_row:
        nx *= 2
    return pl.pallas_call(
        functools.partial(collect_kernel, n, n_row, nx),
        out_shape=(
            jax.ShapeDtypeStruct((layers, tile, width), mid.dtype),
            jax.ShapeDtypeStruct((2, tile, width), mid.dtype),
        ),
        in_specs=[ANY],
        out_specs=(ANY, ANY),
        scratch_shapes=[
            pltpu.VMEM((layers, part, width), mid.dtype),
            pltpu.VMEM((tile, width), mid.dtype),
            pltpu.SemaphoreType.DMA((layers, n - 1)),
            pltpu.SemaphoreType.DMA((layers, n - 1)),
            pltpu.SemaphoreType.DMA((CHUNKS,)),
            pltpu.SemaphoreType.DMA((CHUNKS, nx - 1)),
            pltpu.SemaphoreType.DMA((2, CHUNKS)),
            pltpu.SemaphoreType.DMA((4,)),
        ],
        compiler_params=pltpu.CompilerParams(collective_id=1, has_side_effects=True),
        name="collect",
    )(mid)


def exact(a, b):
    return jnp.dot(a, b, preferred_element_type=F32, precision=lax.Precision.HIGHEST)


def invert_kernel(blocks, inverse):
    count, size, _ = blocks.shape
    r = lax.broadcasted_iota(jnp.int32, (size, size), 0)
    c = lax.broadcasted_iota(jnp.int32, (size, size), 1)
    lows = [blocks[i].astype(F32) for i in range(count)]
    found = []
    for low in lows:
        found.append(jnp.where(r == c, 1.0 / jnp.where(r == c, low, 1.0), 0.0))
    half = 1
    while half < size:
        keep = (r // (2 * half) == c // (2 * half)) & (r // half > c // half)
        left = [exact(f, jnp.where(keep, low, 0.0)) for f, low in zip(found, lows)]
        found = [f - exact(p, f) for f, p in zip(found, left)]
        half *= 2
    for i in range(count):
        inverse[i] = found[i]


def invert(blocks):
    return pl.pallas_call(
        invert_kernel, out_shape=jax.ShapeDtypeStruct(blocks.shape, F32), name="invert"
    )(blocks)


def apply(low, value):
    high = value.astype(BF16)
    rest = value - high.astype(F32)
    middle = rest.astype(BF16)
    last = (rest - middle.astype(F32)).astype(BF16)
    dot = functools.partial(jnp.dot, preferred_element_type=F32)
    return dot(low, high) + (dot(low, middle) + dot(low, last))


def substitute(low, inverse, first, right):
    tile = low.shape[0]
    found = []
    for i in range(tile // BLOCK):
        rows = slice(i * BLOCK, (i + 1) * BLOCK)
        value = right[rows]
        for j in range(i):
            value = value - apply(low[rows, j * BLOCK : (j + 1) * BLOCK], found[j])
        found.append(exact(inverse[first + i], value))
    return jnp.concatenate(found, axis=0).astype(BF16)


def solve_kernel(place, diag, inverse, panels, cast, rhs, out, both):
    tile = diag.shape[1]
    here = place[0]
    top = substitute(diag.at[0], inverse, 0, cast[0].astype(F32))
    both[:tile] = top
    right = cast[1].astype(F32) - jnp.dot(diag[1], top, preferred_element_type=F32)
    both[tile:] = substitute(diag.at[2], inverse, tile // BLOCK, right)
    for m in range(rhs.shape[0]):
        update = jnp.dot(panels[m], both[...], preferred_element_type=F32)
        out[m] = (rhs[m].astype(F32) - update).astype(BF16)

    @pl.when(here == 0)
    def _():
        out[0] = both[:tile]

    @pl.when(here == 1)
    def _():
        out[0] = both[tile:]


def solve(here, diag, inverse, panels, cast, rhs):
    layers, tile, width = rhs.shape
    wide = min(512, width)

    def whole(shape):
        return pl.BlockSpec(shape, lambda j, place: (0,) * len(shape))

    return pl.pallas_call(
        solve_kernel,
        out_shape=jax.ShapeDtypeStruct(rhs.shape, BF16),
        grid_spec=pltpu.PrefetchScalarGridSpec(
            num_scalar_prefetch=1,
            grid=(width // wide,),
            in_specs=[
                whole(diag.shape),
                whole(inverse.shape),
                whole(panels.shape),
                pl.BlockSpec((2, tile, wide), lambda j, place: (0, 0, j)),
                pl.BlockSpec((layers, tile, wide), lambda j, place: (0, 0, j)),
            ],
            out_specs=pl.BlockSpec((layers, tile, wide), lambda j, place: (0, 0, j)),
            scratch_shapes=[pltpu.VMEM((2 * tile, wide), BF16)],
        ),
        compiler_params=pltpu.CompilerParams(vmem_limit_bytes=VMEM_LIMIT),
        name="solve",
    )(here, diag, inverse, panels, cast, rhs)


def body(n, n_row, lower, rhs, tile_map):
    tile = lower.shape[2]
    here = lax.axis_index("row")
    mine = lower[0]
    roots = jnp.stack(
        [
            jnp.where(here == 0, mine[0, :, 0], 0),
            jnp.where(here == 1, mine[0, :, 0], 0),
            jnp.where(here == 1, mine[0, :, 1], 0),
        ]
    ).astype(BF16)
    roots = lax.psum(roots, "row")
    diag = lax.all_gather(roots, "col", axis=2, tiled=True)
    layers = mine.shape[0]
    panels = lax.all_gather(mine, "col", axis=3, tiled=True).reshape(layers, tile, 2 * tile)
    count = tile // BLOCK
    blocks = jnp.stack(
        [
            jnp.tril(diag[k, i * BLOCK : (i + 1) * BLOCK, i * BLOCK : (i + 1) * BLOCK])
            for k in (0, 2)
            for i in range(count)
        ]
    )
    inverse = invert(blocks)
    mid = permute(spread(n, rhs[0]), tile_map, tile)
    moved, cast = collect(n, n_row, mid, tile)
    place = jnp.reshape(here, (1,)).astype(jnp.int32)
    return solve(place, diag, inverse, panels, cast, moved)[None]


def solution(mesh):
    placed = (P("row", None, None, None, "col"), P("row", None, None, "col"), P())
    return jax.shard_map(
        functools.partial(body, mesh.shape["col"], mesh.shape["row"]),
        mesh=mesh,
        in_specs=placed,
        out_specs=P("row", None, None, "col"),
        check_vma=False,
    )
```

time: 624 us -> 331 us (0.53); the launches traced: 614 us -> 330 us
  Pallas kernels: 0 us -> 229 us
  waiting for transfers between devices: 285 us -> 72.4 us
  local copies, waits for them, and re-layouts: 150 us -> 8.01 us
  other arithmetic: 116 us -> 7.05 us
  matrix products: 34.4 us -> 0 us
  starting transfers between devices: 13.7 us -> 0.08 us
    pallas_call x0 -> x5, Pallas kernels: none -> 229 us  [the longest x1 98.3 us: spread(): pl.pallas_call(functools.partial(spread_kernel, n), out_shape=jax.ShapeDt...]
    all_to_all x2 -> x0, waiting for transfers between devices: 149 us -> none  [the longest x1 107 us: body(): lax.all_to_all(rhs, 'col', split_axis=2, concat_axis=3, tiled=True)]
    another operation x4 -> x2, other arithmetic: 81.9 us -> 1.57 us  [the longest x1 0.79 us: body(): jnp.stack([jnp.where(here == 0, mine[0, :, 0], 0), jnp.where(here == 1, m...]
    psum x2 -> x1, waiting for transfers between devices: 136 us -> 71.6 us  [body(): roots = lax.psum(roots, 'row')]
    select_n x1 -> x0, local copies, waits for them, and re-layouts: 39.9 us -> none  [reorder(): return jnp.take(tiles, tile_map, axis=3).reshape(shape)]
    another operation x14 -> x0, matrix products: 24.1 us -> none  [body(): jax.scipy.linalg.solve_triangular(mine, work[0], lower=True)]
    all_to_all x3 -> x0, local copies, waits for them, and re-layouts: 23.6 us -> none  [the longest x2 19.3 us: body(): lax.all_to_all(rhs, 'col', split_axis=2, concat_axis=3, tiled=True)]
    another operation x27 -> x0, local copies, waits for them, and re-layouts: 19.4 us -> none  [body(): jax.scipy.linalg.solve_triangular(mine, work[0], lower=True)]
  transfers between devices with their start and end apart: 5 -> 3, of which waited for: 4 -> 1; matrix products, arithmetic and copies ran while one was open for 33% -> 2% of each run, Pallas kernels for 0% -> 60%
where the time goes in v1:
time: 331 us; the launch traced here: 330 us
  Pallas kernels  229 us (69%)
  waiting for transfers between devices  72.4 us (22%)
  between operations  13.2 us (4%)
  local copies, waits for them, and re-layouts  8.01 us (2%)
  other arithmetic  7.05 us (2%)
    pallas_call x1, Pallas kernels, spread(): pl.pallas_call(functools.partial(spread_kernel, n), out_shape=jax.ShapeDt...  98.3 us
    pallas_call x1, Pallas kernels, collect(): pl.pallas_call(functools.partial(collect_kernel, n, n_row, nx), out_shape...  81.3 us
    psum x1, waiting for transfers between devices, body(): roots = lax.psum(roots, 'row')  71.6 us
    pallas_call x1, Pallas kernels, solve(): pl.pallas_call(solve_kernel, out_shape=jax.ShapeDtypeStruct(rhs.shape, BF...  29.9 us
    pallas_call x1, Pallas kernels, permute(): pl.pallas_call(permute_kernel, out_shape=jax.ShapeDtypeStruct(mid.shape,...  11.6 us
    pallas_call x1, Pallas kernels, invert(): pl.pallas_call(invert_kernel, out_shape=jax.ShapeDtypeStruct(blocks.shape...  8.04 us
  transfers between devices with their start and end apart: 3, of which 1 were waited for; matrix products, arithmetic and copies ran while one was open for 2% of the time, Pallas kernels for 60%

profile of v1, /device:TPU:25, one launch (start us, length us, event | category | flops | bytes accessed | tf_op | source)
XLA Modules:
  0.0 329.8 jit_solution(8140162686523633422)
XLA Ops:
  6.5 0.0 all-reduce.2.cloned.1.call-start
  6.5 1.2 copy.6
  7.8 0.8 pad_maximum_fusion
  8.6 0.0 all-reduce.2.cloned.1.call-update
  8.6 0.0 all-gather.4.cloned.1.call-start
  8.7 71.6 %all-reduce.2.cloned.1.call-done = bf16[3,512,128]{2,1,0:T(8,128)(2,1)} async-done(((bf16[3,512,128]{2,1,0:T(8,128)(2,1)}), bf16[3,512,128]{2,1,0:T(8,128)(2,1)}) %all-reduce.2.cloned.1.call-update) | async-done | bytes 393232 | tf_op jit(solution)/shard_map/psum | solution.py:348
  80.3 0.0 all-gather.4.cloned.1.call-update
  80.3 0.0 all-gather.6.cloned.1.call-start
  80.4 0.7 all-gather.6.cloned.1.call-update
  81.1 98.3 %spread.1.src = bf16[3,128,8192]{2,1,0:T(8,128)(2,1)} custom-call(bf16[3,512,2048]{2,1,0:T(8,128)(2,1)} %bitcast.12), custom_call_target="tpu_custom_call" | custom-call | tf_op jit(solution)/shard_map/spread/pallas_call | solution.py:72
  179.3 11.6 %permute.1.mid = bf16[3,128,8192]{2,1,0:T(8,128)(2,1)} custom-call(s32[16]{0:T(128)} %order.1, bf16[3,128,8192]{2,1,0:T(8,128)(2,1)} %spread.1.src), custom_call_target="tpu_custom_call" | custom-call | tf_op jit(solution)/shard_map/permute/pallas_call | solution.py:94
  191.0 81.3 %collect.1 = (bf16[3,512,2048]{2,1,0:T(8,128)(2,1)}, bf16[2,512,2048]{2,1,0:T(8,128)(2,1)}) custom-call(bf16[3,128,8192]{2,1,0:T(8,128)(2,1)} %permute.1.mid), custom_call_target="tpu_custom_call" | custom-call | tf_op jit(solution)/shard_map/collect/pallas_call | solution.py:217
  272.3 0.0 all-gather.4.cloned.1.call-done.diag
  272.3 0.8 fusion.9
  273.1 0.8 fusion.10
  273.9 0.8 fusion.11
  274.6 0.8 fusion.12
  275.4 0.8 fusion.13
  276.2 0.8 fusion.14
  277.0 0.8 fusion.15
  277.8 0.8 fusion.16.blocks
  278.5 0.0 copy-start
  278.5 0.7 copy-done
  279.2 8.0 %invert.1.inverse = f32[8,128,128]{2,1,0:T(8,128)} custom-call(bf16[8,128,128]{2,1,0:T(8,128)(2,1)} %copy-done), custom_call_target="tpu_custom_call" | custom-call | tf_op jit(solution)/shard_map/invert/pallas_call | solution.py:263
  287.3 0.0 all-gather.6.cloned.1.call-done
  287.3 6.1 %reshape.71.panels = bf16[3,512,1024]{2,1,0:T(8,128)(2,1)} reshape(bf16[1,3,512,2,512]{4,3,2,1,0:T(2,128)(2,1)} %all-gather.6.cloned.1.call-done) | data formatting | bytes 6291456 | tf_op jit(solution)/shard_map/reshape | solution.py:351
  293.4 29.9 %solve.1 = bf16[3,512,2048]{2,1,0:T(8,128)(2,1)} custom-call(s32[1]{0:T(128)} %bitcast.place, bf16[3,512,512]{2,1,0:T(8,128)(2,1)} %all-gather.4.cloned.1.call-done.diag, f32[8,128,128]{2,1,0:T(8,128)} %invert.1.inverse, bf16[3,512,1024]{2,1,0:T(8,128)(2,1)} %reshape.71.panels, bf16[2,512,2048]{2,1,0:T(8,128)(2,1)} %get-tuple-element.7.cast, ...), custom_call_target="tpu_custom_call" | custom-call | tf_op jit(solution)/shard_map/solve/pallas_call | solution.py:316
  (1 shorter events, 0.0 us)
Async XLA Ops:
  6.5 73.8 %all-reduce.2.cloned.1.call-start = ((), (), s32[]{:S(2)}) async-start(), calls=%async_computation | async-start | bytes 786432 | tf_op jit(solution)/shard_map/psum | solution.py:348
  8.6 263.7 %all-gather.4.cloned.1.call-start = ((), (), s32[]{:S(2)}) async-start(), calls=%async_computation.1 | async-start | bytes 1966080 | tf_op jit(solution)/shard_map/all_gather | solution.py:349
  80.3 206.9 %all-gather.6.cloned.1.call-start = ((), (), s32[]{:S(2)}) async-start(), calls=%async_computation.2 | async-start | bytes 3932160 | tf_op jit(solution)/shard_map/all_gather | solution.py:351
  278.5 0.7 copy-start
Sparse Core Ops, SparseCore 0:
  10.7 69.5 all-reduce.1
  81.9 30.9 all-gather.3
  114.4 47.2 all-gather.5

commit v2 on v1

--- a/solution.py
+++ b/solution.py
@@ -30,14 +30,61 @@
     )
 
 
-def spread_kernel(n, rhs, mid, bounce, send, recv, local):
+def spread_kernel(n, n_row, rhs, mine, mid, panels, diag, bounce, hold, send, recv, psend, precv, dsend, drecv, rsend, rrecv, local):
     me = lax.axis_index("col")
+    row = lax.axis_index("row")
+    chips = n // 2
+    chip, core = me // 2, lax.rem(me, 2)
+    twin = me + 1 - 2 * core
     layers, tile, width = rhs.shape
     part = tile // n
     barrier = pltpu.get_barrier_semaphore()
     for d in range(1, n):
         signal(barrier, col=lax.rem(me + d, n))
-    pl.semaphore_wait(barrier, n - 1)
+
+    @pl.loop(1, n_row)
+    def _(d):
+        signal(barrier, row=lax.rem(row + d, n_row))
+
+    pl.semaphore_wait(barrier, n + n_row - 2)
+
+    def root(slot, d):
+        return remote(
+            mine.at[0, slot // 2],
+            diag.at[me, slot],
+            rsend.at[slot, d - 1],
+            rrecv.at[slot],
+            row=lax.rem(row + d, n_row),
+        )
+
+    def from_root(slots, act):
+        @pl.loop(1, n_row)
+        def _(d):
+            for slot in slots:
+                act(root(slot, d))
+
+    roots = ((0, (0,)), (1, (1, 2)))
+    for owner, slots in roots:
+
+        @pl.when(row == owner)
+        def _(slots=slots):
+            from_root(slots, lambda c: c.start())
+
+    def over(q):
+        return lax.rem(chip + q, chips) * 2 + core
+
+    def cross(source, target, ssem, rsem, q):
+        return remote(source, target.at[me], ssem.at[q], rsem.at[q], col=over(q))
+
+    def share(source, target, ssem, rsem, q):
+        held = lax.rem(chip + chips - q, chips) * 2 + core
+        return remote(
+            source if q == 0 else target.at[held],
+            target.at[held],
+            ssem.at[chips + q],
+            rsem.at[chips + q],
+            col=twin,
+        )
 
     def copy(m, d):
         to = lax.rem(me + d, n)
@@ -49,57 +96,130 @@
             col=to,
         )
 
+    for q in range(1, chips):
+        cross(mine, panels, psend, precv, q).start()
+    share(mine, panels, psend, precv, 0).start()
     for m in range(layers):
         for d in range(1, n):
             copy(m, d).start()
     first = pltpu.make_async_copy(rhs.at[:, pl.ds(me * part, part)], bounce, local.at[0])
     first.start()
+    other = pltpu.make_async_copy(mine, hold, local.at[2])
+    other.start()
     first.wait()
     second = pltpu.make_async_copy(bounce, mid.at[:, :, pl.ds(me * width, width)], local.at[1])
     second.start()
+    other.wait()
+    keep = pltpu.make_async_copy(hold, panels.at[me], local.at[3])
+    keep.start()
+    for owner, slots in roots:
+
+        @pl.when(row == owner)
+        def _(slots=slots):
+            for slot in slots:
+                move = pltpu.make_async_copy(
+                    hold.at[0, slot // 2], diag.at[me, slot], local.at[4 + slot]
+                )
+                move.start()
+                move.wait()
+
+        @pl.when(row != owner)
+        def _(slots=slots):
+            for slot in slots:
+                root(slot, 1).wait_recv()
+
     second.wait()
+    keep.wait()
+    for q in range(1, chips):
+        cross(diag.at[me], diag, dsend, drecv, q).start()
+    share(diag.at[me], diag, dsend, drecv, 0).start()
+    for source, target, ssem, rsem in ((mine, panels, psend, precv), (diag.at[me], diag, dsend, drecv)):
+        for q in range(1, chips):
+            cross(source, target, ssem, rsem, q).wait_recv()
+            share(source, target, ssem, rsem, q).start()
     for m in range(layers):
         for d in range(1, n):
             copy(m, d).wait_recv()
+    for source, target, ssem, rsem in ((mine, panels, psend, precv), (diag.at[me], diag, dsend, drecv)):
+        for q in range(chips):
+            share(source, target, ssem, rsem, q).wait_recv()
+            share(source, target, ssem, rsem, q).wait_send()
+        for q in range(1, chips):
+            cross(source, target, ssem, rsem, q).wait_send()
     for m in range(layers):
         for d in range(1, n):
             copy(m, d).wait_send()
-
-
-def spread(n, rhs):
+    for owner, slots in roots:
+
+        @pl.when(row == owner)
+        def _(slots=slots):
+            from_root(slots, lambda c: c.wait_send())
+
+
+def spread(n, n_row, rhs, mine):
     layers, tile, width = rhs.shape
     part = tile // n
+    deep = mine.shape[-1]
+    dma = pltpu.SemaphoreType.DMA
     return pl.pallas_call(
-        functools.partial(spread_kernel, n),
-        out_shape=jax.ShapeDtypeStruct((layers, part, width * n), rhs.dtype),
-        in_specs=[ANY],
-        out_specs=ANY,
+        functools.partial(spread_kernel, n, n_row),
+        out_shape=(
+            jax.ShapeDtypeStruct((layers, part, width * n), rhs.dtype),
+            jax.ShapeDtypeStruct((n,) + mine.shape, mine.dtype),
+            jax.ShapeDtypeStruct((n, 3, tile, deep), mine.dtype),
+        ),
+        in_specs=[ANY, ANY],
+        out_specs=(ANY, ANY, ANY),
         scratch_shapes=[
             pltpu.VMEM((layers, part, width), rhs.dtype),
-            pltpu.SemaphoreType.DMA((layers, n - 1)),
-            pltpu.SemaphoreType.DMA((layers, n - 1)),
-            pltpu.SemaphoreType.DMA((2,)),
+            pltpu.VMEM(mine.shape, mine.dtype),
+            dma((layers, n - 1)),
+            dma((layers, n - 1)),
+            dma((n,)),
+            dma((n,)),
+            dma((n,)),
+            dma((n,)),
+            dma((3, n_row - 1)),
+            dma((3,)),
+            dma((7,)),
         ],
         compiler_params=pltpu.CompilerParams(collective_id=0, has_side_effects=True),
         name="spread",
-    )(rhs)
-
-
-def permute_kernel(order, src, dst):
-    dst[...] = src[...]
+    )(rhs, mine)
+
+
+def permute_kernel(tile, order, src, dst, held, load, store):
+    count = order.shape[0]
+
+    def fetch(j):
+        start = pl.multiple_of(order[j] * tile, tile)
+        return pltpu.make_async_copy(src.at[:, :, pl.ds(start, tile)], held.at[j], load.at[j])
+
+    def put(j):
+        return pltpu.make_async_copy(held.at[j], dst.at[:, :, pl.ds(j * tile, tile)], store.at[j])
+
+    for j in range(count):
+        fetch(j).start()
+    for j in range(count):
+        fetch(j).wait()
+        put(j).start()
+    for j in range(count):
+        put(j).wait()
 
 
 def permute(mid, tile_map, tile):
     layers, part, width = mid.shape
+    count = width // tile
     return pl.pallas_call(
-        permute_kernel,
+        functools.partial(permute_kernel, tile),
         out_shape=jax.ShapeDtypeStruct(mid.shape, mid.dtype),
-        grid_spec=pltpu.PrefetchScalarGridSpec(
-            num_scalar_prefetch=1,
-            grid=(width // tile,),
-            in_specs=[pl.BlockSpec((layers, part, tile), lambda j, order: (0, 0, order[j]))],
-            out_specs=pl.BlockSpec((layers, part, tile), lambda j, order: (0, 0, j)),
-        ),
+        in_specs=[pl.BlockSpec(memory_space=pltpu.SMEM), ANY],
+        out_specs=ANY,
+        scratch_shapes=[
+            pltpu.VMEM((count, layers, part, tile), mid.dtype),
+            pltpu.SemaphoreType.DMA((count,)),
+            pltpu.SemaphoreType.DMA((count,)),
+        ],
         name="permute",
     )(tile_map, mid)
 
@@ -241,60 +361,71 @@
     return jnp.dot(a, b, preferred_element_type=F32, precision=lax.Precision.HIGHEST)
 
 
-def invert_kernel(blocks, inverse):
-    count, size, _ = blocks.shape
+def invert(lows):
+    size = lows[0].shape[0]
     r = lax.broadcasted_iota(jnp.int32, (size, size), 0)
     c = lax.broadcasted_iota(jnp.int32, (size, size), 1)
-    lows = [blocks[i].astype(F32) for i in range(count)]
-    found = []
-    for low in lows:
-        found.append(jnp.where(r == c, 1.0 / jnp.where(r == c, low, 1.0), 0.0))
+    found = [jnp.where(r == c, 1.0 / jnp.where(r == c, low, 1.0), 0.0) for low in lows]
     half = 1
     while half < size:
         keep = (r // (2 * half) == c // (2 * half)) & (r // half > c // half)
         left = [exact(f, jnp.where(keep, low, 0.0)) for f, low in zip(found, lows)]
         found = [f - exact(p, f) for f, p in zip(found, left)]
         half *= 2
-    for i in range(count):
-        inverse[i] = found[i]
-
-
-def invert(blocks):
-    return pl.pallas_call(
-        invert_kernel, out_shape=jax.ShapeDtypeStruct(blocks.shape, F32), name="invert"
-    )(blocks)
-
-
-def apply(low, value):
+    return found
+
+
+def terms(value):
     high = value.astype(BF16)
     rest = value - high.astype(F32)
     middle = rest.astype(BF16)
-    last = (rest - middle.astype(F32)).astype(BF16)
-    dot = functools.partial(jnp.dot, preferred_element_type=F32)
-    return dot(low, high) + (dot(low, middle) + dot(low, last))
+    return high, middle, (rest - middle.astype(F32)).astype(BF16)
 
 
 def substitute(low, inverse, first, right):
-    tile = low.shape[0]
-    found = []
+    tile = right.shape[0]
+    found, pieces = [], []
     for i in range(tile // BLOCK):
-        rows = slice(i * BLOCK, (i + 1) * BLOCK)
-        value = right[rows]
-        for j in range(i):
-            value = value - apply(low[rows, j * BLOCK : (j + 1) * BLOCK], found[j])
-        found.append(exact(inverse[first + i], value))
-    return jnp.concatenate(found, axis=0).astype(BF16)
-
-
-def solve_kernel(place, diag, inverse, panels, cast, rhs, out, both):
-    tile = diag.shape[1]
+        value = right[i * BLOCK : (i + 1) * BLOCK]
+        if i:
+            left = low[i * BLOCK : (i + 1) * BLOCK, : i * BLOCK]
+            for t in range(3):
+                known = jnp.concatenate([p[t] for p in pieces], axis=0)
+                value = value - jnp.dot(left, known, preferred_element_type=F32)
+        value = exact(inverse[first + i], value)
+        found.append(value.astype(BF16))
+        pieces.append(terms(value))
+    return jnp.concatenate(found, axis=0)
+
+
+def solve_kernel(place, diag, panels, cast, rhs, out, both, full, tiles, inverse):
+    n, layers, _, tile, deep = panels.shape
+    count = tile // BLOCK
     here = place[0]
-    top = substitute(diag.at[0], inverse, 0, cast[0].astype(F32))
+
+    @pl.when(pl.program_id(0) == 0)
+    def _():
+        for s in range(n):
+            for k in range(3):
+                tiles[k, :, s * deep : (s + 1) * deep] = diag[s, k]
+            for m in range(layers):
+                for k in range(2):
+                    at = k * tile + s * deep
+                    full[m, :, at : at + deep] = panels[s, m, k]
+        lows = []
+        for k in (0, 2):
+            for i in range(count):
+                at = slice(i * BLOCK, (i + 1) * BLOCK)
+                lows.append(tiles[k, at, at].astype(F32))
+        for i, value in enumerate(invert(lows)):
+            inverse[i] = value
+
+    top = substitute(tiles.at[0], inverse, 0, cast[0].astype(F32))
     both[:tile] = top
-    right = cast[1].astype(F32) - jnp.dot(diag[1], top, preferred_element_type=F32)
-    both[tile:] = substitute(diag.at[2], inverse, tile // BLOCK, right)
-    for m in range(rhs.shape[0]):
-        update = jnp.dot(panels[m], both[...], preferred_element_type=F32)
+    right = cast[1].astype(F32) - jnp.dot(tiles[1], top, preferred_element_type=F32)
+    both[tile:] = substitute(tiles.at[2], inverse, count, right)
+    for m in range(layers):
+        update = jnp.dot(full[m], both[...], preferred_element_type=F32)
         out[m] = (rhs[m].astype(F32) - update).astype(BF16)
 
     @pl.when(here == 0)
@@ -306,12 +437,17 @@
         out[0] = both[tile:]
 
 
-def solve(here, diag, inverse, panels, cast, rhs):
+def solve(here, diag, panels, cast, rhs):
     layers, tile, width = rhs.shape
     wide = min(512, width)
 
     def whole(shape):
-        return pl.BlockSpec(shape, lambda j, place: (0,) * len(shape))
+        return pl.BlockSpec(
+            shape, lambda j, place: (0,) * len(shape), pipeline_mode=pl.Buffered(1)
+        )
+
+    def columns(count):
+        return pl.BlockSpec((count, tile, wide), lambda j, place: (0, 0, j))
 
     return pl.pallas_call(
         solve_kernel,
@@ -319,49 +455,28 @@
         grid_spec=pltpu.PrefetchScalarGridSpec(
             num_scalar_prefetch=1,
             grid=(width // wide,),
-            in_specs=[
-                whole(diag.shape),
-                whole(inverse.shape),
-                whole(panels.shape),
-                pl.BlockSpec((2, tile, wide), lambda j, place: (0, 0, j)),
-                pl.BlockSpec((layers, tile, wide), lambda j, place: (0, 0, j)),
+            in_specs=[whole(diag.shape), whole(panels.shape), columns(2), columns(layers)],
+            out_specs=columns(layers),
+            scratch_shapes=[
+                pltpu.VMEM((2 * tile, wide), BF16),
+                pltpu.VMEM((layers, tile, 2 * tile), BF16),
+                pltpu.VMEM((3, tile, tile), BF16),
+                pltpu.VMEM((2 * tile // BLOCK, BLOCK, BLOCK), F32),
             ],
-            out_specs=pl.BlockSpec((layers, tile, wide), lambda j, place: (0, 0, j)),
-            scratch_shapes=[pltpu.VMEM((2 * tile, wide), BF16)],
         ),
         compiler_params=pltpu.CompilerParams(vmem_limit_bytes=VMEM_LIMIT),
         name="solve",
-    )(here, diag, inverse, panels, cast, rhs)
+    )(here, diag, panels, cast, rhs)
 
 
 def body(n, n_row, lower, rhs, tile_map):
     tile = lower.shape[2]
     here = lax.axis_index("row")
-    mine = lower[0]
-    roots = jnp.stack(
-        [
-            jnp.where(here == 0, mine[0, :, 0], 0),
-            jnp.where(here == 1, mine[0, :, 0], 0),
-            jnp.where(here == 1, mine[0, :, 1], 0),
-        ]
-    ).astype(BF16)
-    roots = lax.psum(roots, "row")
-    diag = lax.all_gather(roots, "col", axis=2, tiled=True)
-    layers = mine.shape[0]
-    panels = lax.all_gather(mine, "col", axis=3, tiled=True).reshape(layers, tile, 2 * tile)
-    count = tile // BLOCK
-    blocks = jnp.stack(
-        [
-            jnp.tril(diag[k, i * BLOCK : (i + 1) * BLOCK, i * BLOCK : (i + 1) * BLOCK])
-            for k in (0, 2)
-            for i in range(count)
-        ]
-    )
-    inverse = invert(blocks)
-    mid = permute(spread(n, rhs[0]), tile_map, tile)
-    moved, cast = collect(n, n_row, mid, tile)
+    mine = jnp.transpose(lower[0], (0, 2, 1, 3))
+    mid, panels, diag = spread(n, n_row, rhs[0], mine)
+    moved, cast = collect(n, n_row, permute(mid, tile_map, tile), tile)
     place = jnp.reshape(here, (1,)).astype(jnp.int32)
-    return solve(place, diag, inverse, panels, cast, moved)[None]
+    return solve(place, diag, panels, cast, moved)[None]
 
 
 def solution(mesh):

time: 331 us -> 227 us (0.69)
  waiting for transfers between devices: 72.4 us -> 0 us
  between operations: 13.2 us -> 0.03 us
  other arithmetic: 7.05 us -> 0 us
  local copies, waits for them, and re-layouts: 8.01 us -> 2.11 us
  Pallas kernels: 229 us -> 225 us
    psum x1 -> x0, waiting for transfers between devices: 71.6 us -> none  [body(): roots = lax.psum(roots, 'row')]
    pallas_call x3 -> x2, Pallas kernels: 118 us -> 105 us  [the longest x1 99.3 us: spread(): pl.pallas_call(functools.partial(spread_kernel, n, n_row), out_shape=(jax...]
    pallas_call x1, Pallas kernels: 29.9 us -> 37.1 us  [solve(): pl.pallas_call(solve_kernel, out_shape=jax.ShapeDtypeStruct(rhs.shape, BF...]
    reshape x1 -> x0, local copies, waits for them, and re-layouts: 6.08 us -> none  [body(): lax.all_gather(mine, 'col', axis=3, tiled=True)]
    unnamed x7 -> x0, other arithmetic: 5.45 us -> none
  transfers between devices with their start and end apart: 3 -> 0, of which waited for: 1 -> 0; matrix products, arithmetic and copies ran while one was open for 2% -> 0% of each run, Pallas kernels for 60% -> 0%
where the time goes in v2:
time: 227 us
  Pallas kernels  225 us (99%)
    pallas_call x1, Pallas kernels, spread(): pl.pallas_call(functools.partial(spread_kernel, n, n_row), out_shape=(jax...  99.3 us
    pallas_call x1, Pallas kernels, collect(): pl.pallas_call(functools.partial(collect_kernel, n, n_row, nx), out_shape...  82.4 us
    pallas_call x1, Pallas kernels, solve(): pl.pallas_call(solve_kernel, out_shape=jax.ShapeDtypeStruct(rhs.shape, BF...  37.1 us
    pallas_call x1, Pallas kernels, permute(): pl.pallas_call(functools.partial(permute_kernel, tile), out_shape=jax.Sha...  6.11 us

profile of v2, /device:TPU:25, one launch (start us, length us, event | category | flops | bytes accessed | tf_op | source)
XLA Modules:
  0.0 227.0 jit_solution(6312011487390889924)
XLA Ops:
  0.0 2.1 copy.6
  2.1 99.3 %spread.1 = (bf16[3,128,8192]{2,1,0:T(8,128)(2,1)}, bf16[4,3,2,512,128]{4,3,2,1,0:T(8,128)(2,1)}, bf16[4,3,512,128]{3,2,1,0:T(8,128)(2,1)}) custom-call(bf16[3,512,2048]{2,1,0:T(8,128)(2,1)} %bitcast.8, bf16[3,2,512,128]{3,2,1,0:T(8,128)(2,1)} %bitcast.9), custom_call_target="tpu_custom_call" | custom-call | tf_op jit(solution)/shard_map/spread/pallas_call | solution.py:164
  101.4 6.1 %permute.1.mid = bf16[3,128,8192]{2,1,0:T(8,128)(2,1)} custom-call(s32[16]{0:T(128)} %order.1, bf16[3,128,8192]{2,1,0:T(8,128)(2,1)} %get-tuple-element.12.src), custom_call_target="tpu_custom_call" | custom-call | tf_op jit(solution)/shard_map/permute/pallas_call | solution.py:213
  107.5 82.4 %collect.1 = (bf16[3,512,2048]{2,1,0:T(8,128)(2,1)}, bf16[2,512,2048]{2,1,0:T(8,128)(2,1)}) custom-call(bf16[3,128,8192]{2,1,0:T(8,128)(2,1)} %permute.1.mid), custom_call_target="tpu_custom_call" | custom-call | tf_op jit(solution)/shard_map/collect/pallas_call | solution.py:337
  189.9 37.1 %solve.1 = bf16[3,512,2048]{2,1,0:T(8,128)(2,1)} custom-call(s32[1]{0:T(128)} %bitcast.place, bf16[4,3,512,128]{3,2,1,0:T(8,128)(2,1)} %get-tuple-element.10.diag, bf16[4,3,2,512,128]{4,3,2,1,0:T(8,128)(2,1)} %get-tuple-element.11.panels, bf16[2,512,2048]{2,1,0:T(8,128)(2,1)} %get-tuple-element.13.cast, bf16[3,512,2048]{2,1,0:T(8,128)(2,1)} %get-tuple-element.14.rhs), custom_call_target="tpu_custom_call" | custom-call | tf_op jit(solution)/shard_map/solve/pallas_call | solution.py:452
